TPU v7x, 32 devices: a whole 2x2x4 slice. The times are simulated.
32 devices in a mesh: leaf: 8 (over z, x), blk: 4 (over y, core).
Axes of the slice: x: 2, y: 2, z: 4, core: 2. Of those that a mesh axis runs over, the one named last changes fastest.
Arguments:
- desc_panel: bfloat16 [256, 384, 128], P(('leaf', 'blk')), may hold values from -18 to 18
- row_map: int32 [256, 3], P(('leaf', 'blk')), may hold values from 0 to 55, as said below
- anc_order: int32 [8], replicated, may hold values from 0 to 7, as said below
- anc_below: int32 [8, 12], replicated, may hold values from 32 to 55, as said below
- anc_panel: float32 [8, 4, 4, 128, 512], P('leaf', None, 'blk'), may hold values from -6 to 27, as said below
Outputs:
- chol_panel: float32 [8, 4, 4, 128, 512], P('leaf', None, 'blk')
Inputs may be any that keep to these rules, and one draw needn't show every extreme that they name: `row_map`: entry 0 of each row is a column block of one ancestor; the other entries are distinct entries of that ancestor's row of anc_below. Over the descendants of one device, entry 0 names the column blocks of any one ancestor at most 2 times, and of some ancestor exactly 2 times. `anc_order`: each leaf index holds a different column range. `anc_below`: each row holds 12 distinct indices. `anc_panel`: the leading 512 rows of each ancestor's panel are symmetric, and the leading block of S stays positive definite.
All inputs are finite; a program needn't handle non-finite values.
Results may differ from a plain program's by a relative error of at most 0.0003.
Values may be sent and summed in bfloat16 or wider, within the bound.
A program may use at most 192 MiB of HBM per device.

v0:
```python
import jax
import jax.numpy as jnp
from jax import lax
from jax.sharding import PartitionSpec as P

SLOTS = 2
slot_group = 16


def leaf_owner(ranges, anc_order):
    leaves = jnp.arange(anc_order.shape[0], dtype=jnp.int32)
    return jnp.sum(jnp.where(anc_order[None, :] == ranges[:, None], leaves[None, :], 0), axis=1)


def block_positions(block_ids, owner_leaf, anc_order, anc_below, column_blocks, position_count):
    column_base = anc_order[owner_leaf] * column_blocks
    relative = block_ids - column_base[:, None]
    in_columns = (relative >= 0) & (relative < column_blocks)
    below_ids = anc_below[owner_leaf]
    matching = block_ids[:, :, None] == below_ids[:, None, :]
    offsets = column_blocks + jnp.arange(below_ids.shape[1], dtype=jnp.int32)
    below_place = jnp.sum(jnp.where(matching, offsets[None, None, :], 0), axis=2)
    located = jnp.any(matching, axis=2)
    return jnp.where(in_columns, relative, jnp.where(located, below_place, position_count))


def place_blocks(running, group_place, group_products):
    return running + jnp.einsum(
        "kq,kxy->qxy", group_place, group_products, precision=lax.Precision.HIGHEST
    )


def shards(desc_panel, row_map, anc_order, anc_below, anc_panel):
    leaf_count = lax.axis_size("leaf")
    blk_count = lax.axis_size("blk")
    desc_count, block_count = row_map.shape
    block_rows = anc_panel.shape[3]
    panel_width = anc_panel.shape[4]
    wide_desc = desc_panel.shape[2]
    column_blocks = panel_width // block_rows
    position_count = column_blocks + anc_below.shape[1]
    slot_count = leaf_count * SLOTS
    group_count = slot_count // slot_group
    owner_leaf = leaf_owner(row_map[:, 0] // column_blocks, anc_order)
    positions = block_positions(
        row_map, owner_leaf, anc_order, anc_below, column_blocks, position_count
    )
    desc_index = jnp.arange(desc_count, dtype=jnp.int32)
    same_owner = owner_leaf[:, None] == owner_leaf[None, :]
    earlier = desc_index[None, :] < desc_index[:, None]
    ranking = jnp.sum(same_owner & earlier, axis=1)
    slot_of = owner_leaf * SLOTS + ranking
    matches = slot_of[None, :] == jnp.arange(slot_count, dtype=jnp.int32)[:, None]
    filled = jnp.any(matches, axis=1)
    chosen = jnp.sum(jnp.where(matches, desc_index[None, :], 0), axis=1)
    picked = jnp.where(filled, chosen, desc_count)
    slot_codes = jnp.where(filled[:, None], positions[chosen], position_count).reshape(
        leaf_count, SLOTS, block_count
    )
    send_rows = jnp.take(desc_panel, picked, axis=0, mode="fill", fill_value=0)
    send_rows = send_rows.reshape(leaf_count, SLOTS, block_count * block_rows, wide_desc)
    received, received_codes = (
        lax.all_to_all(send_rows, "leaf", split_axis=0, concat_axis=0, tiled=True),
        lax.all_to_all(
            slot_codes.astype(jnp.bfloat16), "leaf", split_axis=0, concat_axis=0, tiled=True
        ),
    )
    slot_data = received.reshape(group_count, slot_group, block_count * block_rows, wide_desc)

    def accumulate(running, element):
        group_data, group_place = element
        products = jnp.einsum(
            "kaw,kyw->kay",
            group_data,
            group_data[:, :block_rows],
            preferred_element_type=jnp.float32,
        )
        products = products.reshape(slot_group * block_count, block_rows, block_rows)
        return (place_blocks(running, group_place, products), None)

    codes_int = received_codes.astype(jnp.int32).reshape(slot_count, block_count)
    target = codes_int * column_blocks + codes_int[:, :1]
    placing = (
        target[:, :, None]
        == jnp.arange(position_count * column_blocks, dtype=jnp.int32)[None, None, :]
    ).astype(jnp.float32)
    placing = placing.reshape(group_count, slot_group * block_count, position_count * column_blocks)
    initial = jnp.zeros((position_count * column_blocks, block_rows, block_rows), jnp.float32)
    running, _ = lax.scan(accumulate, initial, (slot_data, placing))
    update = running.reshape(position_count, column_blocks, block_rows, block_rows).transpose(
        0, 2, 1, 3
    )
    update = update.reshape(position_count // blk_count, blk_count, block_rows, panel_width)
    local_rows = anc_panel[0]
    mine = lax.axis_index("blk")
    marker = (jnp.arange(blk_count, dtype=jnp.int32) == mine).astype(jnp.float32)
    combined = update - local_rows * marker[None, :, None, None]
    summed = lax.psum(combined, "blk")
    diagonal = -summed.reshape(position_count * block_rows, panel_width)[:panel_width]
    own_rows = -lax.dynamic_slice_in_dim(summed, mine, 1, 1)
    lower_factor = jnp.linalg.cholesky(diagonal)
    panel_rows = own_rows.reshape(-1, panel_width)
    solved = jax.scipy.linalg.solve_triangular(lower_factor, panel_rows.T, lower=True).T
    return solved.reshape(anc_panel.shape)


def solution(mesh):
    in_specs = (
        P(("leaf", "blk"), None, None),
        P(("leaf", "blk"), None),
        P(),
        P(),
        P("leaf", None, "blk", None, None),
    )
    out_specs = P("leaf", None, "blk", None, None)
    return jax.shard_map(shards, mesh=mesh, in_specs=in_specs, out_specs=out_specs, check_vma=False)
```

profile of v0, /device:TPU:0, one launch (start us, length us, event | category | flops | bytes accessed | tf_op | source)
XLA Modules:
  0.0 327.3 jit_solution(11401863305329569041)
XLA Ops:
  6.5 0.8 fusion.45
  7.3 0.8 select_reduce_fusion.5
  8.5 0.8 copy.53
  9.4 1.3 gather_fusion
  10.7 1.2 gather_fusion.1
  11.9 0.9 compare_reduce_fusion
  12.8 0.9 fusion.40
  14.0 0.6 gather_fusion.2
  14.8 0.7 copy.58
  15.5 7.3 %all-to-all-start = ((bf16[8,2,3]{2,1,0:T(2,128)(2,1)}), bf16[8,2,3]{2,1,0:T(2,128)(2,1)S(1)}, u32[]{:S(2)}, u32[]{:S(2)}) async-start(bf16[8,2,3]{2,1,0:T(2,128)(2,1)} %copy.58), calls=%async_computation | async-start | bytes 8192 | tf_op jit(solution)/shard_map/all_to_all | solution.py:64
  22.8 0.9 gather_fusion.3
  23.7 1.3 broadcast_select_fusion
  25.0 4.1 %all-to-all-done = bf16[8,2,3]{2,1,0:T(2,128)(2,1)S(1)} async-done(((bf16[8,2,3]{2,1,0:T(2,128)(2,1)}), bf16[8,2,3]{2,1,0:T(2,128)(2,1)S(1)}, u32[]{:S(2)}, u32[]{:S(2)}) %all-to-all-start) | async-done | bytes 128 | tf_op jit(solution)/shard_map/all_to_all | solution.py:64
  29.2 3.6 %all-to-all-start.1 = ((bf16[8,2,384,128]{3,2,1,0:T(8,128)(2,1)}), bf16[8,2,384,128]{3,2,1,0:T(8,128)(2,1)S(1)}, u32[]{:S(2)}, u32[]{:S(2)}) async-start(bf16[8,2,384,128]{3,2,1,0:T(8,128)(2,1)} %broadcast_select_fusion), calls=%async_computation.1 | async-start | bytes 3145728 | tf_op jit(solution)/shard_map/all_to_all | solution.py:63
  32.8 1.6 copy.62
  34.8 33.9 %all-to-all-done.1 = bf16[8,2,384,128]{3,2,1,0:T(8,128)(2,1)S(1)} async-done(((bf16[8,2,384,128]{3,2,1,0:T(8,128)(2,1)}), bf16[8,2,384,128]{3,2,1,0:T(8,128)(2,1)S(1)}, u32[]{:S(2)}, u32[]{:S(2)}) %all-to-all-start.1) | async-done | bytes 1572896 | tf_op jit(solution)/shard_map/all_to_all | solution.py:63
  68.7 0.6 fusion.12
  69.3 6.0 %fusion.3 = f32[16,128,4,128]{3,0,1,2:T(8,128)} fusion(f32[48,128,128]{2,1,0:T(8,128)S(1)} %bitcast.107, s32[16,4]{0,1:T(4,128)S(1)} %multiply_add_fusion, s32[48]{0:T(128)S(1)} %add.130), kind=kOutput, calls=%fused_computation.10 | convolution fusion | flops 603982848 | bytes 7340480 | tf_op jit(solution)/shard_map/while/body/eval_jaxpr/kq,kxy->qxy/dot_general | solution.py:28
  75.3 5.7 %copy.61 = f32[16,128,4,128]{1,3,2,0:T(8,128)} copy(f32[16,128,4,128]{3,0,1,2:T(8,128)} %fusion.3) | data formatting | bytes 8388608 | tf_op jit(solution)/shard_map/transpose | solution.py:90
  80.9 4.7 %multiply_subtract_fusion = f32[4,4,128,512]{2,3,1,0:T(8,128)} fusion(f32[4,4,128,512]{2,3,1,0:T(8,128)} %bitcast.106, f32[4]{0:T(128)S(1)} %compare_convert_fusion, f32[4,128,512]{1,2,0:T(8,128)S(1)} %copy.62), kind=kLoop, calls=%fused_computation.6 | loop fusion | flops 2097152 | bytes 9437200 | tf_op jit(solution)/shard_map/sub | solution.py:97
  85.7 84.5 %all-reduce.3.cloned.1.call-done = f32[4,4,128,512]{2,3,1,0:T(8,128)} async-done(((f32[4,4,128,512]{2,3,1,0:T(8,128)}), f32[4,4,128,512]{2,3,1,0:T(8,128)}) %all-reduce.3.cloned.1.call-update) | async-done | bytes 4194320 | tf_op jit(solution)/shard_map/psum | solution.py:98
  170.1 1.3 slice_negate_fusion
  171.4 0.7 copy.63
  172.1 1.0 copy.84
  173.2 1.6 copy.64
  174.7 0.2 fusion.6
  175.0 1.0 copy-done.2
  175.9 11.7 %cholesky.104 = f32[128,128]{1,0:T(8,128)S(1)} custom-call(f32[128,128]{1,0:T(8,128)S(1)} %cholesky.266), custom_call_target="Cholesky" | custom-call | tf_op jit(solution)/shard_map/jit(cholesky)/cholesky | solution.py:101
  187.8 9.8 %custom-call.31 = f32[1,128,128]{1,2,0:T(8,128)S(1)} custom-call(f32[1,128,128]{2,1,0:T(8,128)S(1)} %get-tuple-element.44), custom_call_target="InvertDiagBlocksLowerTriangular" | custom-call | tf_op jit(solution)/shard_map/jit(cholesky)/cholesky | solution.py:101
  197.6 1.2 constant_dynamic-update-slice_fusion.3
  198.9 1.3 convolution_subtract_fusion.3
  200.1 11.9 %cholesky.217 = f32[128,128]{1,0:T(8,128)S(1)} custom-call(f32[128,128]{1,0:T(8,128)S(1)} %cholesky.270), custom_call_target="Cholesky" | custom-call | tf_op jit(solution)/shard_map/jit(cholesky)/cholesky | solution.py:101
  212.0 0.7 compare_reduce_fusion.3
  212.7 0.6 compare_reduce_fusion.4
  213.4 9.8 %custom-call.32 = f32[1,128,128]{1,2,0:T(8,128)S(1)} custom-call(f32[1,128,128]{2,1,0:T(8,128)S(1)} %get-tuple-element.41), custom_call_target="InvertDiagBlocksLowerTriangular" | custom-call | tf_op jit(solution)/shard_map/jit(cholesky)/cholesky | solution.py:101
  223.2 0.3 convolution_dynamic-update-slice_fusion
  223.4 1.3 convolution_subtract_fusion.4
  224.7 11.7 %cholesky.238 = f32[128,128]{1,0:T(8,128)S(1)} custom-call(f32[128,128]{1,0:T(8,128)S(1)} %cholesky.275), custom_call_target="Cholesky" | custom-call | tf_op jit(solution)/shard_map/jit(cholesky)/cholesky | solution.py:101
  236.5 0.7 compare_reduce_fusion.2
  237.2 9.8 %custom-call.33 = f32[1,128,128]{1,2,0:T(8,128)S(1)} custom-call(f32[1,128,128]{2,1,0:T(8,128)S(1)} %get-tuple-element.38), custom_call_target="InvertDiagBlocksLowerTriangular" | custom-call | tf_op jit(solution)/shard_map/jit(cholesky)/cholesky | solution.py:101
  247.2 1.2 convolution_subtract_fusion.5
  248.5 11.9 %cholesky.255 = f32[128,128]{1,0:T(8,128)S(1)} custom-call(f32[128,128]{1,0:T(8,128)S(1)} %convolution_subtract_fusion.5), custom_call_target="Cholesky" | custom-call | tf_op jit(solution)/shard_map/jit(cholesky)/cholesky | solution.py:101
  260.4 0.6 compare_reduce_fusion.1
  263.8 7.9 %while.1 = (s32[]{:T(128)}, f32[512,512]{1,0:T(8,128)S(1)}, s32[4,2]{0,1:T(2,128)S(1)}, f32[4,128,128]{2,1,0:T(8,128)S(1)}, s32[]{:T(128)}) while((s32[]{:T(128)}, f32[512,512]{1,0:T(8,128)S(1)}, s32[4,2]{0,1:T(2,128)S(1)}, f32[4,128,128]{2,1,0:T(8,128)S(1)}, s32[]{:T(128)}) %tuple.30), condition=%wide.while_cond, body=%wide.while_body.sunk | while | flops 2 | bytes 131181 | solution.py:103
  263.9 0.5 fusion.57
  264.4 1.4 bitcast_dynamic-update-slice_fusion.2
  265.8 0.5 fusion.57
  266.4 1.4 bitcast_dynamic-update-slice_fusion.2
  267.8 0.5 fusion.57
  268.3 1.4 bitcast_dynamic-update-slice_fusion.2
  269.8 0.5 fusion.57
  270.3 1.4 bitcast_dynamic-update-slice_fusion.2
  271.7 39.3 %custom-call.34 = f32[4,128,128]{1,2,0:T(8,128)S(1)} custom-call(f32[4,128,128]{2,1,0:T(8,128)S(1)} %get-tuple-element.24), custom_call_target="InvertDiagBlocksLowerTriangular" | custom-call | tf_op jit(solution)/shard_map/jit(_solve_triangular)/triangular_solve | solution.py:103
  311.0 1.3 dynamic-slice_negate_fusion
  312.3 0.3 copy.65
  312.7 0.3 copy.66
  313.0 0.4 fusion.17
  313.4 1.2 convolution_subtract_fusion.1
  314.6 0.4 fusion.30
  315.1 1.3 convolution_subtract_fusion
  316.4 0.4 fusion.28
  316.8 1.6 convolution_subtract_fusion.2
  318.4 0.4 fusion.27
  318.9 1.3 copy.72
  (53 shorter events, 2.4 us)
Async XLA Ops:
  6.5 16.3 %copy-start = (bf16[8,384,128]{2,1,0:T(8,128)(2,1)S(1)}, bf16[8,384,128]{2,1,0:T(8,128)(2,1)}, u32[]{:S(2)}) copy-start(bf16[8,384,128]{2,1,0:T(8,128)(2,1)} %param.5) | copy-start | bytes 2359300
  15.5 13.7 %all-to-all-start = ((bf16[8,2,3]{2,1,0:T(2,128)(2,1)}), bf16[8,2,3]{2,1,0:T(2,128)(2,1)S(1)}, u32[]{:S(2)}, u32[]{:S(2)}) async-start(bf16[8,2,3]{2,1,0:T(2,128)(2,1)} %copy.58), calls=%async_computation | async-start | bytes 8192 | tf_op jit(solution)/shard_map/all_to_all | solution.py:64
  29.2 39.5 %all-to-all-start.1 = ((bf16[8,2,384,128]{3,2,1,0:T(8,128)(2,1)}), bf16[8,2,384,128]{3,2,1,0:T(8,128)(2,1)S(1)}, u32[]{:S(2)}, u32[]{:S(2)}) async-start(bf16[8,2,384,128]{3,2,1,0:T(8,128)(2,1)} %broadcast_select_fusion), calls=%async_computation.1 | async-start | bytes 3145728 | tf_op jit(solution)/shard_map/all_to_all | solution.py:63
  32.7 137.4 %all-reduce.3.cloned.1.call-start = ((), (), s32[]{:S(2)}) async-start(), calls=%async_computation.2 | async-start | bytes 8388608 | tf_op jit(solution)/shard_map/psum | solution.py:98
  174.9 1.0 copy-start.2
  271.7 39.3 %copy-start.1 = (f32[512,512]{1,0:T(8,128)}, f32[512,512]{1,0:T(8,128)S(1)}, u32[]{:S(2)}) copy-start(f32[512,512]{1,0:T(8,128)S(1)} %get-tuple-element.101) | copy-start | bytes 3145732
Sparse Core Ops, SparseCore 0:
  85.8 84.3 all-reduce.2
where the time goes:
time: 333 us; the launch traced here: 327 us
  other arithmetic  132 us (40%)
  waiting for transfers between devices  123 us (37%)
  local copies, waits for them, and re-layouts  27.7 us (8%)
  matrix products  17.8 us (5%)
  between operations  16.6 us (5%)
  starting transfers between devices  10.9 us (3%)
    psum x1, waiting for transfers between devices, shards(): summed = lax.psum(combined, 'blk')  84.5 us
    another operation x15, other arithmetic, shards(): lower_factor = jnp.linalg.cholesky(diagonal)  79.4 us
    another operation x3, other arithmetic, shards(): jax.scipy.linalg.solve_triangular(lower_factor, panel_rows.T, lower=True)  39.4 us
    all_to_all x1, waiting for transfers between devices, shards(): lax.all_to_all(send_rows, 'leaf', split_axis=0, concat_axis=0, tiled=True)  33.9 us
    another operation x12, local copies, waits for them, and re-layouts  7.81 us
    all_to_all x1, starting transfers between devices, shards(): lax.all_to_all(slot_codes.astype(jnp.bfloat16), 'leaf', split_axis=0, con...  7.28 us
  transfers between devices with their start and end apart: 3, of which 3 were waited for; matrix products, arithmetic and copies ran while one was open for 1% of the time, Pallas kernels for 0%

commit v1 on v0

--- a/solution.py
+++ b/solution.py
@@ -95,7 +95,8 @@
     mine = lax.axis_index("blk")
     marker = (jnp.arange(blk_count, dtype=jnp.int32) == mine).astype(jnp.float32)
     combined = update - local_rows * marker[None, :, None, None]
-    summed = lax.psum(combined, "blk")
+    parts = lax.all_gather(combined, "blk")
+    summed = jnp.sum(parts, axis=0)
     diagonal = -summed.reshape(position_count * block_rows, panel_width)[:panel_width]
     own_rows = -lax.dynamic_slice_in_dim(summed, mine, 1, 1)
     lower_factor = jnp.linalg.cholesky(diagonal)

time: 333 us -> 371 us (1.11)
  waiting for transfers between devices: 123 us -> 143 us
  local copies, waits for them, and re-layouts: 27.7 us -> 36.7 us
  other arithmetic: 132 us -> 139 us
    all_gather x0 -> x1, waiting for transfers between devices: none -> 105 us  [shards(): parts = lax.all_gather(combined, 'blk')]
    psum x1 -> x0, waiting for transfers between devices: 84.5 us -> none  [shards(): summed = lax.psum(combined, 'blk')]
    reduce_sum x0 -> x1, other arithmetic: none -> 10.3 us  [shards(): summed = jnp.sum(parts, axis=0)]
    sub x0 -> x1, local copies, waits for them, and re-layouts: none -> 5.68 us  [shards(): combined = update - local_rows * marker[None, :, None, None]]
where the time goes in v1:
time: 371 us; the launch traced here: 365 us
  waiting for transfers between devices  143 us (39%)
  other arithmetic  139 us (37%)
  local copies, waits for them, and re-layouts  36.7 us (10%)
  matrix products  18 us (5%)
  between operations  16.6 us (4%)
  starting transfers between devices  10.9 us (3%)
    all_gather x1, waiting for transfers between devices, shards(): parts = lax.all_gather(combined, 'blk')  105 us
    another operation x15, other arithmetic, shards(): lower_factor = jnp.linalg.cholesky(diagonal)  79.2 us
    another operation x3, other arithmetic, shards(): jax.scipy.linalg.solve_triangular(lower_factor, panel_rows.T, lower=True)  39.4 us
    all_to_all x1, waiting for transfers between devices, shards(): lax.all_to_all(send_rows, 'leaf', split_axis=0, concat_axis=0, tiled=True)  33.9 us
    reduce_sum x1, other arithmetic, shards(): summed = jnp.sum(parts, axis=0)  10.3 us
    another operation x12, local copies, waits for them, and re-layouts  8.39 us
  transfers between devices with their start and end apart: 3, of which 3 were waited for; matrix products, arithmetic and copies ran while one was open for 1% of the time, Pallas kernels for 0%

profile of v1, /device:TPU:0, one launch (start us, length us, event | category | flops | bytes accessed | tf_op | source)
XLA Modules:
  0.0 364.7 jit_solution(12782355200673824989)
XLA Ops:
  6.5 0.8 fusion.45
  7.3 0.8 select_reduce_fusion.5
  8.5 0.8 copy.55
  9.4 1.3 gather_fusion
  10.7 1.2 gather_fusion.1
  11.9 0.9 compare_reduce_fusion
  12.8 0.9 fusion.40
  14.0 0.6 gather_fusion.2
  14.8 0.7 copy.60
  15.5 7.3 %all-to-all-start = ((bf16[8,2,3]{2,1,0:T(2,128)(2,1)}), bf16[8,2,3]{2,1,0:T(2,128)(2,1)S(1)}, u32[]{:S(2)}, u32[]{:S(2)}) async-start(bf16[8,2,3]{2,1,0:T(2,128)(2,1)} %copy.60), calls=%async_computation | async-start | bytes 8192 | tf_op jit(solution)/shard_map/all_to_all | solution.py:64
  22.8 0.9 gather_fusion.3
  23.7 1.3 broadcast_select_fusion
  25.0 4.1 %all-to-all-done = bf16[8,2,3]{2,1,0:T(2,128)(2,1)S(1)} async-done(((bf16[8,2,3]{2,1,0:T(2,128)(2,1)}), bf16[8,2,3]{2,1,0:T(2,128)(2,1)S(1)}, u32[]{:S(2)}, u32[]{:S(2)}) %all-to-all-start) | async-done | bytes 128 | tf_op jit(solution)/shard_map/all_to_all | solution.py:64
  29.2 3.6 all-to-all-start.1
  32.8 1.6 copy.64
  34.8 33.9 %all-to-all-done.1 = bf16[8,2,384,128]{3,2,1,0:T(8,128)(2,1)S(1)} async-done(((bf16[8,2,384,128]{3,2,1,0:T(8,128)(2,1)}), bf16[8,2,384,128]{3,2,1,0:T(8,128)(2,1)S(1)}, u32[]{:S(2)}, u32[]{:S(2)}) %all-to-all-start.1) | async-done | bytes 1572896 | tf_op jit(solution)/shard_map/all_to_all | solution.py:63
  68.7 0.6 fusion.12
  69.3 6.0 %fusion.3 = f32[16,128,4,128]{3,0,1,2:T(8,128)} fusion(f32[48,128,128]{2,1,0:T(8,128)S(1)} %bitcast.107, s32[16,4]{0,1:T(4,128)S(1)} %multiply_add_fusion, s32[48]{0:T(128)S(1)} %add.128), kind=kOutput, calls=%fused_computation.10 | convolution fusion | flops 603982848 | bytes 7340480 | tf_op jit(solution)/shard_map/while/body/eval_jaxpr/kq,kxy->qxy/dot_general | solution.py:28
  75.3 5.2 %copy.63 = f32[16,128,4,128]{1,3,2,0:T(8,128)} copy(f32[16,128,4,128]{3,0,1,2:T(8,128)} %fusion.3) | data formatting | bytes 8388608 | tf_op jit(solution)/shard_map/transpose | solution.py:90
  80.5 4.7 %multiply_subtract_fusion = f32[1,4,4,128,512]{3,4,2,1,0:T(8,128)} fusion(f32[1,4,4,128,512]{3,4,2,1,0:T(8,128)} %bitcast.106, f32[4]{0:T(128)S(1)} %compare_convert_fusion, f32[4,128,512]{1,2,0:T(8,128)S(1)} %copy.64), kind=kLoop, calls=%fused_computation.6 | loop fusion | flops 2097152 | bytes 9437200 | tf_op jit(solution)/shard_map/sub | solution.py:97
  85.2 5.7 %copy.65 = f32[1,4,4,128,512]{4,3,2,1,0:T(8,128)} copy(f32[1,4,4,128,512]{3,4,2,1,0:T(8,128)} %multiply_subtract_fusion) | data formatting | bytes 8388608 | tf_op jit(solution)/shard_map/sub | solution.py:97
  90.9 104.9 %all-gather.2.cloned.1.call-done = f32[4,4,4,128,512]{4,3,2,1,0:T(8,128)} async-done(((f32[1,4,4,128,512]{4,3,2,1,0:T(8,128)}), f32[4,4,4,128,512]{4,3,2,1,0:T(8,128)}) %all-gather.2.cloned.1.call-update) | async-done | bytes 16777232 | tf_op jit(solution)/shard_map/all_gather | solution.py:98
  195.8 10.3 %reduce_sum.58 = f32[4,4,128,512]{3,2,1,0:T(8,128)} reduce(f32[4,4,4,128,512]{4,3,2,1,0:T(8,128)} %all-gather.2.cloned.1.call-done, f32[]{:T(128)} %constant.201.clone.1), dimensions={0}, to_apply=%region_6.7 | reduce | flops 3145728 | bytes 20971524 | tf_op jit(solution)/shard_map/reduce_sum | solution.py:99
  206.1 1.3 slice.153
  207.8 0.7 copy.67
  208.5 1.0 copy.91
  209.5 1.6 copy.68
  211.3 1.0 copy-done.3
  212.3 11.7 %cholesky.104 = f32[128,128]{1,0:T(8,128)S(1)} custom-call(f32[128,128]{1,0:T(8,128)S(1)} %cholesky.266), custom_call_target="Cholesky" | custom-call | tf_op jit(solution)/shard_map/jit(cholesky)/cholesky | solution.py:102
  224.2 9.8 %custom-call.31 = f32[1,128,128]{1,2,0:T(8,128)S(1)} custom-call(f32[1,128,128]{2,1,0:T(8,128)S(1)} %get-tuple-element.44), custom_call_target="InvertDiagBlocksLowerTriangular" | custom-call | tf_op jit(solution)/shard_map/jit(cholesky)/cholesky | solution.py:102
  234.0 1.2 constant_dynamic-update-slice_fusion.3
  235.2 1.3 convolution_subtract_fusion.3
  236.5 11.9 %cholesky.217 = f32[128,128]{1,0:T(8,128)S(1)} custom-call(f32[128,128]{1,0:T(8,128)S(1)} %cholesky.270), custom_call_target="Cholesky" | custom-call | tf_op jit(solution)/shard_map/jit(cholesky)/cholesky | solution.py:102
  248.4 0.6 compare_reduce_fusion.3
  249.1 0.7 compare_reduce_fusion.4
  249.8 9.8 %custom-call.32 = f32[1,128,128]{1,2,0:T(8,128)S(1)} custom-call(f32[1,128,128]{2,1,0:T(8,128)S(1)} %get-tuple-element.41), custom_call_target="InvertDiagBlocksLowerTriangular" | custom-call | tf_op jit(solution)/shard_map/jit(cholesky)/cholesky | solution.py:102
  259.9 1.3 convolution_subtract_fusion.4
  261.2 11.7 %cholesky.238 = f32[128,128]{1,0:T(8,128)S(1)} custom-call(f32[128,128]{1,0:T(8,128)S(1)} %cholesky.275), custom_call_target="Cholesky" | custom-call | tf_op jit(solution)/shard_map/jit(cholesky)/cholesky | solution.py:102
  272.9 0.7 compare_reduce_fusion.2
  273.6 9.8 %custom-call.33 = f32[1,128,128]{1,2,0:T(8,128)S(1)} custom-call(f32[1,128,128]{2,1,0:T(8,128)S(1)} %get-tuple-element.38), custom_call_target="InvertDiagBlocksLowerTriangular" | custom-call | tf_op jit(solution)/shard_map/jit(cholesky)/cholesky | solution.py:102
  283.6 1.4 convolution_subtract_fusion.5
  285.0 11.7 %cholesky.255 = f32[128,128]{1,0:T(8,128)S(1)} custom-call(f32[128,128]{1,0:T(8,128)S(1)} %convolution_subtract_fusion.5), custom_call_target="Cholesky" | custom-call | tf_op jit(solution)/shard_map/jit(cholesky)/cholesky | solution.py:102
  296.8 0.6 compare_reduce_fusion.1
  300.1 8.5 %while.1 = (s32[]{:T(128)}, f32[512,512]{1,0:T(8,128)S(1)}, s32[4,2]{0,1:T(2,128)S(1)}, f32[4,128,128]{2,1,0:T(8,128)S(1)}, s32[]{:T(128)}) while((s32[]{:T(128)}, f32[512,512]{1,0:T(8,128)S(1)}, s32[4,2]{0,1:T(2,128)S(1)}, f32[4,128,128]{2,1,0:T(8,128)S(1)}, s32[]{:T(128)}) %tuple.30), condition=%wide.while_cond, body=%wide.while_body.sunk | while | flops 2 | bytes 131181 | solution.py:104
  300.2 0.6 fusion.57
  300.8 1.4 bitcast_dynamic-update-slice_fusion.2
  302.3 0.6 fusion.57
  302.9 1.4 bitcast_dynamic-update-slice_fusion.2
  304.4 0.6 fusion.57
  305.0 1.4 bitcast_dynamic-update-slice_fusion.2
  306.6 0.6 fusion.57
  307.2 1.4 bitcast_dynamic-update-slice_fusion.2
  308.6 39.3 %custom-call.34 = f32[4,128,128]{1,2,0:T(8,128)S(1)} custom-call(f32[4,128,128]{2,1,0:T(8,128)S(1)} %get-tuple-element.24), custom_call_target="InvertDiagBlocksLowerTriangular" | custom-call | tf_op jit(solution)/shard_map/jit(_solve_triangular)/triangular_solve | solution.py:104
  347.9 1.3 constant_dynamic-slice_fusion.1
  349.7 0.3 copy.69
  350.0 0.3 copy.70
  350.3 0.4 fusion.17
  350.8 1.2 convolution_subtract_fusion.1
  352.0 0.4 fusion.30
  352.4 1.3 convolution_subtract_fusion
  353.8 0.4 fusion.28
  354.2 1.6 convolution_subtract_fusion.2
  355.8 0.4 fusion.27
  356.3 1.3 copy.76
  (61 shorter events, 3.7 us)
Async XLA Ops:
  6.5 16.3 %copy-start = (bf16[8,384,128]{2,1,0:T(8,128)(2,1)S(1)}, bf16[8,384,128]{2,1,0:T(8,128)(2,1)}, u32[]{:S(2)}) copy-start(bf16[8,384,128]{2,1,0:T(8,128)(2,1)} %param.5) | copy-start | bytes 2359300
  15.5 13.7 %all-to-all-start = ((bf16[8,2,3]{2,1,0:T(2,128)(2,1)}), bf16[8,2,3]{2,1,0:T(2,128)(2,1)S(1)}, u32[]{:S(2)}, u32[]{:S(2)}) async-start(bf16[8,2,3]{2,1,0:T(2,128)(2,1)} %copy.60), calls=%async_computation | async-start | bytes 8192 | tf_op jit(solution)/shard_map/all_to_all | solution.py:64
  29.2 39.5 %all-to-all-start.1 = ((bf16[8,2,384,128]{3,2,1,0:T(8,128)(2,1)}), bf16[8,2,384,128]{3,2,1,0:T(8,128)(2,1)S(1)}, u32[]{:S(2)}, u32[]{:S(2)}) async-start(bf16[8,2,384,128]{3,2,1,0:T(8,128)(2,1)} %broadcast_select_fusion), calls=%async_computation.1 | async-start | bytes 3145728 | tf_op jit(solution)/shard_map/all_to_all | solution.py:63
  32.7 163.0 %all-gather.2.cloned.1.call-start = ((), (), s32[]{:S(2)}) async-start(), calls=%async_computation.2 | async-start | bytes 20971520 | tf_op jit(solution)/shard_map/all_gather | solution.py:98
  211.3 1.0 copy-start.3
  308.6 39.3 %copy-start.2 = (f32[512,512]{1,0:T(8,128)}, f32[512,512]{1,0:T(8,128)S(1)}, u32[]{:S(2)}) copy-start(f32[512,512]{1,0:T(8,128)S(1)} %get-tuple-element.102) | copy-start | bytes 3145732
  353.7 3.8 %copy-start.1 = (bf16[8,384,128]{2,1,0:T(8,128)(2,1)S(1)}, bf16[8,384,128]{2,1,0:T(8,128)(2,1)}, u32[]{:S(2)}) copy-start(bf16[8,384,128]{2,1,0:T(8,128)(2,1)} %param.5) | copy-start | bytes 2359300
Sparse Core Ops, SparseCore 0:
  91.0 104.7 all-gather.1
